TPU v7x, 512 devices: a whole 4x4x16 slice. The times are simulated.
512 devices in a mesh: tm: 128 (over x, z, y_hi), cuts: 4 (over y_lo, core).
Axes of the slice: x: 4, y: 4 (y_hi: 2, y_lo: 2; y = y_hi * 2 + y_lo), z: 16, core: 2. Of those that a mesh axis runs over, the one named last changes fastest.
Arguments:
- start_image: float32 [512, 2, 128, 256], P(('cuts', 'tm')), parts along dimension 0, may hold values from -6 to 6
- sensitivity: bfloat16 [32, 2, 128, 256], P('cuts'), parts along dimension 0, may hold values from -2 to 2
- kspace: bfloat16 [512, 8, 2, 128, 256], P(('cuts', 'tm')), parts along dimension 0, may hold values from -6 to 6
- sampled: int32 [512, 8, 256], P(('cuts', 'tm')), parts along dimension 0, may hold values from 0 to 1
- offsets: int32 [8, 2], P('cuts'), parts along dimension 0, may hold values from 0 to 15
Outputs:
- reconstruction: float32 [512, 2, 128, 256], P(('cuts', 'tm')), parts along dimension 0
There are 4 independent parts, one for each index of `cuts`. A program takes and returns all parts, laid end to end along the dimension named above; each array names one. Nothing has to cross between parts.
All inputs are finite; a program needn't handle non-finite values. Where the computation divides by a largest or mean magnitude, that divisor is 1e-20 or more.
Results may differ from a plain program's by a relative error of at most 0.0037.
Values sent between devices are 32-bit elements; how exact they have to be, the bound alone decides.
A program may use at most 64 MiB of HBM per device.

v0:
```python
import functools
import math

import jax
import jax.numpy as jnp
import numpy as np
from jax import lax
from jax.experimental import pallas as pl
from jax.experimental.pallas import tpu as pltpu
from jax.sharding import PartitionSpec as P

BS = 16
LANES = 128
PER_TILE = LANES // BS
ROWS = 32
shrink_ratio = 0.5
epsilon = 1e-06
HIGHEST = lax.Precision.HIGHEST
F32 = jnp.float32
BF16 = jnp.bfloat16


def dft_matrices(length):
    indices = np.arange(length, dtype=np.int64)
    phases = (indices[:, None] * indices[None, :]) % length
    angles = phases.astype(np.float32) * np.float32(2.0 * math.pi / length)
    norm_scale = np.float32(1.0 / math.sqrt(length))
    cosine = jnp.asarray(np.cos(angles) * norm_scale).astype(BF16)
    sine = jnp.asarray(np.sin(angles) * norm_scale).astype(BF16)
    ahead = jnp.block([[cosine, -sine], [sine, cosine]])
    back = jnp.block([[cosine, sine], [-sine, cosine]])
    return ahead, back


def swap_groups(x):
    rows, lanes = x.shape
    row = lax.broadcasted_iota(jnp.int32, x.shape, 0)
    lane = lax.broadcasted_iota(jnp.int32, x.shape, 1)
    for bit in (1, 2, 4):
        low_row = (row & bit) == 0
        low_lane = (lane & (bit * BS)) == 0
        from_below = pltpu.roll(pltpu.roll(x, rows - bit, 0), bit * BS, 1)
        from_above = pltpu.roll(pltpu.roll(x, bit, 0), lanes - bit * BS, 1)
        x = jnp.where(low_row == low_lane, x, jnp.where(low_row, from_below, from_above))
    return x


def kernel(
    sizes, iters, newton,
    start, sens, kspace, sampled, offsets, ahead, back,
    out,
    field, grad, sums_src, sums, casorati_src, casorati, shrunk_src, shrunk,
    send_sems, recv_sems,
):
    nx, nz, ny = sizes
    count = nx * nz * ny
    coils, _, width, length = sens.shape
    halves = length // LANES
    per_row = length // BS
    me = lax.axis_index("tm")
    my_x, my_z, my_y = me // (nz * ny), (me // ny) % nz, me % ny
    barrier = pltpu.get_barrier_semaphore()

    def peers(act):
        def at_distance(i, skip_self):
            hop = nz // 2 + (1 - 2 * (i % 2)) * ((i + 1) // 2)
            z = (my_z + hop) % nz
            for dx in range(nx):
                for dy in range(ny):
                    if skip_self and dx == 0 and dy == 0:
                        continue
                    act((((my_x + dx) % nx) * nz + z) * ny + (my_y + dy) % ny)

        def body(i, carry):
            at_distance(i, False)
            return carry

        lax.fori_loop(0, nz - 1, body, 0)
        at_distance(nz - 1, True)

    peers(lambda peer: pl.semaphore_signal(barrier, inc=1, device_id={"tm": peer}))

    field[...] = start[...]
    weight = sampled[...].astype(F32)[:, None, :]

    def exchange(src_of, dst, phase, it):
        def send(peer):
            pltpu.make_async_remote_copy(
                src_ref=src_of(peer),
                dst_ref=dst.at[it, me],
                send_sem=send_sems.at[phase, it],
                recv_sem=recv_sems.at[phase, it],
                device_id={"tm": peer},
            ).start()

        peers(send)

    def all_of(dst, phase, it):
        whole = dst.at[it, pl.ds(0, count - 1)]
        return pltpu.make_async_remote_copy(
            src_ref=whole, dst_ref=whole, send_sem=send_sems.at[phase, it],
            recv_sem=recv_sems.at[phase, it], device_id={"tm": me},
        )

    def iteration(it, carry):
        def chunk(c, acc):
            num, den = acc
            r0 = pl.multiple_of(c * ROWS, ROWS)
            here = pl.ds(r0, ROWS)
            sr = sens[:, 0, here, :].astype(F32)
            si = sens[:, 1, here, :].astype(F32)

            def spectra(re, im):
                cr = (sr * re - si * im).astype(BF16).reshape(coils * ROWS, length)
                ci = (sr * im + si * re).astype(BF16).reshape(coils * ROWS, length)
                spec = jnp.dot(
                    jnp.concatenate([cr, ci], axis=1), ahead[...], preferred_element_type=F32
                )
                return (
                    spec[:, :length].reshape(coils, ROWS, length),
                    spec[:, length:].reshape(coils, ROWS, length),
                )

            fr, fi = spectra(field[0, here, :], field[1, here, :])
            mr = (weight * (fr - kspace[:, 0, here, :].astype(F32))).astype(BF16)
            mi = (weight * (fi - kspace[:, 1, here, :].astype(F32))).astype(BF16)
            misfit = jnp.concatenate(
                [mr.reshape(coils * ROWS, length), mi.reshape(coils * ROWS, length)], axis=1
            )
            image = jnp.dot(misfit, back[...], preferred_element_type=F32)
            br = image[:, :length].reshape(coils, ROWS, length)
            bi = image[:, length:].reshape(coils, ROWS, length)
            gr = jnp.sum(sr * br + si * bi, axis=0)
            gi = jnp.sum(sr * bi - si * br, axis=0)
            grad[0, here, :] = gr
            grad[1, here, :] = gi
            num = num + jnp.sum((gr * gr + gi * gi).reshape(ROWS // 8, 8, length), axis=0)
            pr, pi = spectra(gr, gi)
            power = jnp.sum(weight * (pr * pr + pi * pi), axis=0)
            den = den + jnp.sum(power.reshape(ROWS // 8, 8, length), axis=0)
            return num, den

        zero = jnp.zeros((8, length), F32)
        num, den = lax.fori_loop(0, width // ROWS, chunk, (zero, zero))

        def fold(v):
            v = jnp.sum(v, axis=0, keepdims=True)
            v = sum(v[:, h * LANES : (h + 1) * LANES] for h in range(halves))
            return v + pltpu.roll(v, LANES // 2, 1)

        first = lax.broadcasted_iota(jnp.int32, (1, LANES), 1) < LANES // 2
        mine = jnp.where(first, fold(num), fold(den))
        sums_src[it] = mine
        sums[it, me] = mine

        @pl.when(it == 0)
        def _():
            pl.semaphore_wait(barrier, count - 1)

        exchange(lambda peer: sums_src.at[it], sums, 0, it)
        all_of(sums, 0, it).wait_recv()
        total = jnp.sum(sums[it], axis=0)
        num_all = jnp.sum(jnp.where(first, total, 0.0), axis=1, keepdims=True)
        den_all = jnp.sum(jnp.where(first, 0.0, total), axis=1, keepdims=True)
        step_length = num_all / (den_all + epsilon)

        shift_x, shift_y = offsets[it, 0], offsets[it, 1]
        for p in range(2):
            moved = field[p] - step_length * grad[p]
            rolled = pltpu.roll(pltpu.roll(moved, shift_x, 0), shift_y, 1)
            for h in range(halves):
                swapped = swap_groups(rolled[:, h * LANES : (h + 1) * LANES])
                for g in range(width // 8):
                    u, q = g // 2, g % 2
                    rows = pl.ds(u * per_row + h * PER_TILE, PER_TILE)
                    casorati_src[it, rows, p * 2 + q, :] = swapped[g * 8 : (g + 1) * 8, :]

        exchange(lambda peer: casorati_src.at[it, peer], casorati, 1, it)
        casorati[it, me] = casorati_src[it, me]
        all_of(casorati, 1, it).wait_recv()

        parts = [casorati[it, :, j, :] for j in range(4)]
        contract_last = (((1,), (1,)), ((), ()))
        full = jnp.concatenate(parts, axis=1)
        gram = lax.dot_general(
            full, full, contract_last, precision=HIGHEST, preferred_element_type=F32
        )
        frames = gram.shape[0]
        eye = (
            lax.broadcasted_iota(jnp.int32, gram.shape, 0)
            == lax.broadcasted_iota(jnp.int32, gram.shape, 1)
        ).astype(F32)
        trace = jnp.sum(jnp.sum(gram * eye, axis=1, keepdims=True), axis=0, keepdims=True)
        level = shrink_ratio * trace / frames + epsilon
        system = gram + level * eye
        bound = jnp.max(jnp.sum(jnp.abs(system), axis=1, keepdims=True), axis=0, keepdims=True)

        def times(a, b):
            return jnp.dot(a, b, precision=HIGHEST, preferred_element_type=F32)

        residual = eye - system / bound
        product = eye + residual
        power = times(residual, residual)
        for step in range(newton - 2):
            both = times(jnp.concatenate([power, product], axis=0), power)
            product = product + both[frames:]
            power = both[:frames]
        product = product + times(product, power)
        scaled = product * (level / bound)
        result = full - times(scaled, full)
        for j in range(4):
            shrunk_src[it, :, j, :] = result[:, j * LANES : (j + 1) * LANES]

        exchange(lambda peer: shrunk_src.at[it, peer], shrunk, 2, it)
        shrunk[it, me] = shrunk_src[it, me]
        all_of(shrunk, 2, it).wait_recv()

        for p in range(2):
            columns = []
            for h in range(halves):
                tiles = []
                for g in range(width // 8):
                    u, q = g // 2, g % 2
                    rows = pl.ds(u * per_row + h * PER_TILE, PER_TILE)
                    tiles.append(shrunk[it, rows, p * 2 + q, :])
                columns.append(swap_groups(jnp.concatenate(tiles, axis=0)))
            placed = jnp.concatenate(columns, axis=1)
            field[p] = pltpu.roll(pltpu.roll(placed, width - shift_x, 0), length - shift_y, 1)

        for phase, dst in enumerate((sums, casorati, shrunk)):
            all_of(dst, phase, it).wait_send()
        return carry

    lax.fori_loop(0, iters, iteration, 0)
    out[...] = field[...]


def body(sizes, start_image, sensitivity, kspace, sampled, offsets):
    iters = offsets.shape[0]
    newton = 4
    _, _, width, length = start_image.shape
    coils = sensitivity.shape[0]
    count = sizes[0] * sizes[1] * sizes[2]
    ahead, back = dft_matrices(length)
    vmem = pl.BlockSpec(memory_space=pltpu.VMEM)
    run = pl.pallas_call(
        functools.partial(kernel, sizes, iters, newton),
        name="reconstruct",
        out_shape=jax.ShapeDtypeStruct((2, width, length), F32),
        in_specs=[vmem, vmem, vmem, vmem, pl.BlockSpec(memory_space=pltpu.SMEM), vmem, vmem],
        out_specs=vmem,
        scratch_shapes=[
            pltpu.VMEM((2, width, length), F32),
            pltpu.VMEM((2, width, length), F32),
            pltpu.VMEM((iters, 1, LANES), F32),
            pltpu.VMEM((iters, count, 1, LANES), F32),
            pltpu.VMEM((iters, count, 4, LANES), F32),
            pltpu.VMEM((iters, count, 4, LANES), F32),
            pltpu.VMEM((iters, count, 4, LANES), F32),
            pltpu.VMEM((iters, count, 4, LANES), F32),
            pltpu.SemaphoreType.DMA((3, iters)),
            pltpu.SemaphoreType.DMA((3, iters)),
        ],
        compiler_params=pltpu.CompilerParams(
            collective_id=0, has_side_effects=True, vmem_limit_bytes=48 * 2**20
        ),
    )
    result = run(start_image[0], sensitivity, kspace[0], sampled[0], offsets, ahead, back)
    return result[None]


def solution(mesh):
    count = mesh.shape["tm"]
    sizes = (4, count // 8, 2) if count >= 64 else (2, count // 4, 2)
    both = ("cuts", "tm")
    placed = (
        P(both, None, None, None),
        P("cuts", None, None, None),
        P(both, None, None, None, None),
        P(both, None, None),
        P("cuts", None),
    )
    return jax.shard_map(
        functools.partial(body, sizes), mesh=mesh, in_specs=placed,
        out_specs=P(both, None, None, None), check_vma=False,
    )
```

profile of v0, /device:TPU:1, one launch (start us, length us, event | category | flops | bytes accessed | tf_op | source)
XLA Modules:
  0.0 118.6 jit_solution(2103352359663014666)
XLA Ops:
  0.0 0.0 copy-start.6
  0.0 0.7 copy-done.6
  0.7 0.0 copy-start
  0.7 1.2 %copy-done = bf16[8,2,128,256]{3,2,1,0:T(8,128)(2,1)S(1)} copy-done((bf16[8,2,128,256]{3,2,1,0:T(8,128)(2,1)S(1)}, bf16[8,2,128,256]{3,2,1,0:T(8,128)(2,1)}, u32[]{:S(2)}) %copy-start) | copy-done | bytes 1048600
  1.9 0.0 copy-start.1
  1.9 1.2 %copy-done.1 = bf16[1,8,2,128,256]{4,3,2,1,0:T(8,128)(2,1)S(1)} copy-done((bf16[1,8,2,128,256]{4,3,2,1,0:T(8,128)(2,1)S(1)}, bf16[1,8,2,128,256]{4,3,2,1,0:T(8,128)(2,1)}, u32[]{:S(2)}) %copy-start.1) | copy-done | bytes 1048600
  3.1 0.0 copy-start.2
  3.1 1.0 copy-done.2
  4.2 0.0 copy-start.3
  4.2 1.0 copy-done.3
  5.2 0.0 copy-start.4
  5.2 0.9 copy-done.4
  6.2 0.0 copy-start.5
  6.2 0.7 copy-done.5
  6.9 111.1 %reconstruct.1 = f32[2,128,256]{2,1,0:T(8,128)S(1)} custom-call(f32[2,128,256]{2,1,0:T(8,128)S(1)} %bitcast.6, bf16[8,2,128,256]{3,2,1,0:T(8,128)(2,1)S(1)} %copy-done, bf16[8,2,128,256]{3,2,1,0:T(8,128)(2,1)S(1)} %bitcast.4, s32[8,256]{1,0:T(8,128)S(1)} %bitcast.7, s32[2,2]{1,0:T(2,128)S(1)} %copy-done.6, bf16[512,512]{1,0:T(8,128)(2,1)S(1)} %copy-done.3, ...), custom_call_target="tpu_custom_call" | custom-call | tf_op jit(solution)/shard_map/reconstruct/pallas_call | solution.py:268
  117.9 0.7 copy.9
Async XLA Ops:
  0.0 0.7 copy-start.6
  0.7 1.2 %copy-start = (bf16[8,2,128,256]{3,2,1,0:T(8,128)(2,1)S(1)}, bf16[8,2,128,256]{3,2,1,0:T(8,128)(2,1)}, u32[]{:S(2)}) copy-start(bf16[8,2,128,256]{3,2,1,0:T(8,128)(2,1)} %sens.1) | copy-start | bytes 3145732
  1.9 1.2 %copy-start.1 = (bf16[1,8,2,128,256]{4,3,2,1,0:T(8,128)(2,1)S(1)}, bf16[1,8,2,128,256]{4,3,2,1,0:T(8,128)(2,1)}, u32[]{:S(2)}) copy-start(bf16[1,8,2,128,256]{4,3,2,1,0:T(8,128)(2,1)} %param.9) | copy-start | bytes 3145732
  3.1 1.0 copy-start.2
  4.2 1.0 copy-start.3
  5.2 0.9 copy-start.4
  6.2 0.7 copy-start.5
where the time goes:
time: 119 us
  Pallas kernels  111 us (93%)
  local copies, waits for them, and re-layouts  7.56 us (6%)
    pallas_call x1, Pallas kernels, body(): run(start_image[0], sensitivity, kspace[0], sampled[0], offsets, ahead, b...  111 us
    unnamed x15, local copies, waits for them, and re-layouts  7.56 us

commit v1 on v0

--- a/solution.py
+++ b/solution.py
@@ -12,10 +12,11 @@
 BS = 16
 LANES = 128
 PER_TILE = LANES // BS
-ROWS = 32
+ROWS = 64
+EARLY = 0
+CLASSES = 2
 shrink_ratio = 0.5
 epsilon = 1e-06
-HIGHEST = lax.Precision.HIGHEST
 F32 = jnp.float32
 BF16 = jnp.bfloat16
 
@@ -47,10 +48,12 @@
 
 def kernel(
     sizes, iters, newton,
-    start, sens, kspace, sampled, offsets, ahead, back,
+    start_hbm, sens_hbm, kspace_hbm, sampled_hbm, offsets, ahead_hbm, back_hbm,
     out,
-    field, grad, sums_src, sums, casorati_src, casorati, shrunk_src, shrunk,
-    send_sems, recv_sems,
+    sens, kspace, sampled, ahead, back,
+    field, grad, sums_src, sums, held_src, held, slope_src, slope,
+    casorati_src, casorati, shrunk_src, shrunk,
+    load_sems, send_sems, recv_sems,
 ):
     nx, nz, ny = sizes
     count = nx * nz * ny
@@ -59,31 +62,51 @@
     per_row = length // BS
     me = lax.axis_index("tm")
     my_x, my_z, my_y = me // (nz * ny), (me // ny) % nz, me % ny
+    plane = nx * ny
+    reach = min(EARLY, nz - 1)
     barrier = pltpu.get_barrier_semaphore()
-
-    def peers(act):
-        def at_distance(i, skip_self):
-            hop = nz // 2 + (1 - 2 * (i % 2)) * ((i + 1) // 2)
-            z = (my_z + hop) % nz
-            for dx in range(nx):
+    loads = [
+        pltpu.make_async_copy(src, dst, load_sems.at[i])
+        for i, (src, dst) in enumerate(
+            (
+                (sampled_hbm, sampled), (start_hbm, field), (sens_hbm, sens),
+                (ahead_hbm, ahead), (kspace_hbm, kspace), (back_hbm, back),
+            )
+        )
+    ]
+    for load in loads:
+        load.start()
+
+    def hop_of(i):
+        return nz // 2 + (1 - 2 * (i % 2)) * ((i + 1) // 2)
+
+    def peers(act, low=0, high=nz, classes=1):
+        span = high - low
+
+        def body(i, carry):
+            z = (my_z + hop_of(low + i % span)) % nz
+            for dx in range(nx // classes):
                 for dy in range(ny):
-                    if skip_self and dx == 0 and dy == 0:
-                        continue
-                    act((((my_x + dx) % nx) * nz + z) * ny + (my_y + dy) % ny)
-
-        def body(i, carry):
-            at_distance(i, False)
+                    if classes == 1:
+                        x = (my_x + dx) % nx
+                    else:
+                        x = i // span + classes * dx
+                    peer = (x * nz + z) * ny + (my_y + dy) % ny
+                    if high < nz:
+                        act(peer)
+                    else:
+                        pl.when(peer != me)(functools.partial(act, peer))
             return carry
 
-        lax.fori_loop(0, nz - 1, body, 0)
-        at_distance(nz - 1, True)
+        lax.fori_loop(0, classes * span, body, 0)
 
     peers(lambda peer: pl.semaphore_signal(barrier, inc=1, device_id={"tm": peer}))
 
-    field[...] = start[...]
+    for load in loads:
+        load.wait()
     weight = sampled[...].astype(F32)[:, None, :]
 
-    def exchange(src_of, dst, phase, it):
+    def exchange(src_of, dst, phase, it, *which):
         def send(peer):
             pltpu.make_async_remote_copy(
                 src_ref=src_of(peer),
@@ -93,10 +116,10 @@
                 device_id={"tm": peer},
             ).start()
 
-        peers(send)
-
-    def all_of(dst, phase, it):
-        whole = dst.at[it, pl.ds(0, count - 1)]
+        peers(send, *which)
+
+    def all_of(dst, phase, it, amount):
+        whole = dst.at[it, pl.ds(0, amount)]
         return pltpu.make_async_remote_copy(
             src_ref=whole, dst_ref=whole, send_sem=send_sems.at[phase, it],
             recv_sem=recv_sems.at[phase, it], device_id={"tm": me},
@@ -158,32 +181,59 @@
             pl.semaphore_wait(barrier, count - 1)
 
         exchange(lambda peer: sums_src.at[it], sums, 0, it)
-        all_of(sums, 0, it).wait_recv()
+
+        shift_x, shift_y = offsets[it, 0], offsets[it, 1]
+
+        def lay_out(image, dst):
+            for p in range(2):
+                rolled = pltpu.roll(pltpu.roll(image[p], shift_x, 0), shift_y, 1)
+                for h in range(halves):
+                    swapped = swap_groups(rolled[:, h * LANES : (h + 1) * LANES])
+                    for g in range(width // 8):
+                        u, q = g // 2, g % 2
+                        rows = pl.ds(u * per_row + h * PER_TILE, PER_TILE)
+                        dst[it, rows, p * 2 + q, :] = swapped[g * 8 : (g + 1) * 8, :]
+
+        lay_out(field, held_src)
+        if reach:
+            exchange(lambda peer: held_src.at[it, peer], held, 1, it, 0, reach)
+        lay_out(grad, slope_src)
+        if reach:
+            exchange(lambda peer: slope_src.at[it, peer], slope, 2, it, 0, reach)
+
+        all_of(sums, 0, it, count - 1).wait_recv()
         total = jnp.sum(sums[it], axis=0)
         num_all = jnp.sum(jnp.where(first, total, 0.0), axis=1, keepdims=True)
         den_all = jnp.sum(jnp.where(first, 0.0, total), axis=1, keepdims=True)
         step_length = num_all / (den_all + epsilon)
 
-        shift_x, shift_y = offsets[it, 0], offsets[it, 1]
-        for p in range(2):
-            moved = field[p] - step_length * grad[p]
-            rolled = pltpu.roll(pltpu.roll(moved, shift_x, 0), shift_y, 1)
-            for h in range(halves):
-                swapped = swap_groups(rolled[:, h * LANES : (h + 1) * LANES])
-                for g in range(width // 8):
-                    u, q = g // 2, g % 2
-                    rows = pl.ds(u * per_row + h * PER_TILE, PER_TILE)
-                    casorati_src[it, rows, p * 2 + q, :] = swapped[g * 8 : (g + 1) * 8, :]
-
-        exchange(lambda peer: casorati_src.at[it, peer], casorati, 1, it)
+        casorati_src[it] = held_src[it] - step_length[None] * slope_src[it]
+        exchange(
+            lambda peer: casorati_src.at[it, peer], casorati, 3, it, reach, nz, CLASSES
+        )
         casorati[it, me] = casorati_src[it, me]
-        all_of(casorati, 1, it).wait_recv()
+        if reach:
+            all_of(held, 1, it, reach * plane).wait_recv()
+            all_of(slope, 2, it, reach * plane).wait_recv()
+        all_of(casorati, 3, it, count - 1 - reach * plane).wait_recv()
+        for k in range(reach):
+            z = (my_z + hop_of(k)) % nz
+            for x in range(nx):
+                rows = pl.ds((x * nz + z) * ny, ny)
+                casorati[it, rows] = held[it, rows] - step_length[None] * slope[it, rows]
 
         parts = [casorati[it, :, j, :] for j in range(4)]
-        contract_last = (((1,), (1,)), ((), ()))
         full = jnp.concatenate(parts, axis=1)
+
+        def split(a):
+            high = a.astype(BF16)
+            return high, (a - high.astype(F32)).astype(BF16)
+
+        full_high, full_low = split(full)
         gram = lax.dot_general(
-            full, full, contract_last, precision=HIGHEST, preferred_element_type=F32
+            jnp.concatenate([full_high, full_low, full_high], axis=1),
+            jnp.concatenate([full_high, full_high, full_low], axis=1),
+            (((1,), (1,)), ((), ())), preferred_element_type=F32,
         )
         frames = gram.shape[0]
         eye = (
@@ -196,7 +246,13 @@
         bound = jnp.max(jnp.sum(jnp.abs(system), axis=1, keepdims=True), axis=0, keepdims=True)
 
         def times(a, b):
-            return jnp.dot(a, b, precision=HIGHEST, preferred_element_type=F32)
+            a_high, a_low = split(a)
+            b_high, b_low = split(b)
+            return jnp.dot(
+                jnp.concatenate([a_high, a_low, a_high], axis=1),
+                jnp.concatenate([b_high, b_high, b_low], axis=0),
+                preferred_element_type=F32,
+            )
 
         residual = eye - system / bound
         product = eye + residual
@@ -211,9 +267,9 @@
         for j in range(4):
             shrunk_src[it, :, j, :] = result[:, j * LANES : (j + 1) * LANES]
 
-        exchange(lambda peer: shrunk_src.at[it, peer], shrunk, 2, it)
+        exchange(lambda peer: shrunk_src.at[it, peer], shrunk, 4, it)
         shrunk[it, me] = shrunk_src[it, me]
-        all_of(shrunk, 2, it).wait_recv()
+        all_of(shrunk, 4, it, count - 1).wait_recv()
 
         for p in range(2):
             columns = []
@@ -227,8 +283,13 @@
             placed = jnp.concatenate(columns, axis=1)
             field[p] = pltpu.roll(pltpu.roll(placed, width - shift_x, 0), length - shift_y, 1)
 
-        for phase, dst in enumerate((sums, casorati, shrunk)):
-            all_of(dst, phase, it).wait_send()
+        early = reach * plane
+        for phase, dst, amount in (
+            (0, sums, count - 1), (1, held, early), (2, slope, early),
+            (3, casorati, count - 1 - early), (4, shrunk, count - 1),
+        ):
+            if amount:
+                all_of(dst, phase, it, amount).wait_send()
         return carry
 
     lax.fori_loop(0, iters, iteration, 0)
@@ -243,23 +304,28 @@
     count = sizes[0] * sizes[1] * sizes[2]
     ahead, back = dft_matrices(length)
     vmem = pl.BlockSpec(memory_space=pltpu.VMEM)
+    hbm = pl.BlockSpec(memory_space=pltpu.HBM)
+    messages = pltpu.VMEM((iters, count, 4, LANES), F32)
     run = pl.pallas_call(
         functools.partial(kernel, sizes, iters, newton),
         name="reconstruct",
         out_shape=jax.ShapeDtypeStruct((2, width, length), F32),
-        in_specs=[vmem, vmem, vmem, vmem, pl.BlockSpec(memory_space=pltpu.SMEM), vmem, vmem],
+        in_specs=[hbm, hbm, hbm, hbm, pl.BlockSpec(memory_space=pltpu.SMEM), hbm, hbm],
         out_specs=vmem,
         scratch_shapes=[
+            pltpu.VMEM(sensitivity.shape, BF16),
+            pltpu.VMEM(kspace.shape[1:], BF16),
+            pltpu.VMEM(sampled.shape[1:], jnp.int32),
+            pltpu.VMEM(ahead.shape, BF16),
+            pltpu.VMEM(back.shape, BF16),
             pltpu.VMEM((2, width, length), F32),
             pltpu.VMEM((2, width, length), F32),
             pltpu.VMEM((iters, 1, LANES), F32),
             pltpu.VMEM((iters, count, 1, LANES), F32),
-            pltpu.VMEM((iters, count, 4, LANES), F32),
-            pltpu.VMEM((iters, count, 4, LANES), F32),
-            pltpu.VMEM((iters, count, 4, LANES), F32),
-            pltpu.VMEM((iters, count, 4, LANES), F32),
-            pltpu.SemaphoreType.DMA((3, iters)),
-            pltpu.SemaphoreType.DMA((3, iters)),
+            *[messages] * 8,
+            pltpu.SemaphoreType.DMA((6,)),
+            pltpu.SemaphoreType.DMA((5, iters)),
+            pltpu.SemaphoreType.DMA((5, iters)),
         ],
         compiler_params=pltpu.CompilerParams(
             collective_id=0, has_side_effects=True, vmem_limit_bytes=48 * 2**20

time: 119 us -> 112 us (0.941)
  the two profiles are of different devices: /device:TPU:1 before, /device:TPU:24 now
where the time goes in v1:
time: 112 us; the launch traced here: 111 us
  Pallas kernels  103 us (92%)
  local copies, waits for them, and re-layouts  7.56 us (7%)
    pallas_call x1, Pallas kernels, body(): run(start_image[0], sensitivity, kspace[0], sampled[0], offsets, ahead, b...  103 us
    unnamed x15, local copies, waits for them, and re-layouts  7.56 us

profile of v1, /device:TPU:24, one launch (start us, length us, event | category | flops | bytes accessed | tf_op | source)
XLA Modules:
  0.0 110.7 jit_solution(6158704183411286249)
XLA Ops:
  0.0 0.0 copy-start.6
  0.0 0.7 copy-done.6
  0.7 0.0 copy-start
  0.7 1.2 %copy-done = bf16[8,2,128,256]{3,2,1,0:T(8,128)(2,1)S(1)} copy-done((bf16[8,2,128,256]{3,2,1,0:T(8,128)(2,1)S(1)}, bf16[8,2,128,256]{3,2,1,0:T(8,128)(2,1)}, u32[]{:S(2)}) %copy-start) | copy-done | bytes 1048600
  1.9 0.0 copy-start.1
  1.9 1.2 %copy-done.1 = bf16[1,8,2,128,256]{4,3,2,1,0:T(8,128)(2,1)S(1)} copy-done((bf16[1,8,2,128,256]{4,3,2,1,0:T(8,128)(2,1)S(1)}, bf16[1,8,2,128,256]{4,3,2,1,0:T(8,128)(2,1)}, u32[]{:S(2)}) %copy-start.1) | copy-done | bytes 1048600
  3.1 0.0 copy-start.2
  3.1 1.0 copy-done.2
  4.2 0.0 copy-start.3
  4.2 1.0 copy-done.3
  5.2 0.0 copy-start.4
  5.2 0.9 copy-done.4
  6.2 0.0 copy-start.5
  6.2 0.7 copy-done.5
  6.9 103.1 %reconstruct.1 = f32[2,128,256]{2,1,0:T(8,128)S(1)} custom-call(f32[2,128,256]{2,1,0:T(8,128)S(1)} %bitcast.6, bf16[8,2,128,256]{3,2,1,0:T(8,128)(2,1)S(1)} %copy-done, bf16[8,2,128,256]{3,2,1,0:T(8,128)(2,1)S(1)} %bitcast.4, s32[8,256]{1,0:T(8,128)S(1)} %bitcast.7, s32[2,2]{1,0:T(2,128)S(1)} %copy-done.6, bf16[512,512]{1,0:T(8,128)(2,1)S(1)} %copy-done.3, ...), custom_call_target="tpu_custom_call" | custom-call | tf_op jit(solution)/shard_map/reconstruct/pallas_call | solution.py:334
  110.0 0.7 copy.9
Async XLA Ops:
  0.0 0.7 copy-start.6
  0.7 1.2 %copy-start = (bf16[8,2,128,256]{3,2,1,0:T(8,128)(2,1)S(1)}, bf16[8,2,128,256]{3,2,1,0:T(8,128)(2,1)}, u32[]{:S(2)}) copy-start(bf16[8,2,128,256]{3,2,1,0:T(8,128)(2,1)} %sens_hbm.1) | copy-start | bytes 3145732
  1.9 1.2 %copy-start.1 = (bf16[1,8,2,128,256]{4,3,2,1,0:T(8,128)(2,1)S(1)}, bf16[1,8,2,128,256]{4,3,2,1,0:T(8,128)(2,1)}, u32[]{:S(2)}) copy-start(bf16[1,8,2,128,256]{4,3,2,1,0:T(8,128)(2,1)} %param.9) | copy-start | bytes 3145732
  3.1 1.0 copy-start.2
  4.2 1.0 copy-start.3
  5.2 0.9 copy-start.4
  6.2 0.7 copy-start.5

commit v2 on v1

--- a/solution.py
+++ b/solution.py
@@ -12,7 +12,7 @@
 BS = 16
 LANES = 128
 PER_TILE = LANES // BS
-ROWS = 64
+ROWS = 128
 EARLY = 0
 CLASSES = 2
 shrink_ratio = 0.5
@@ -48,9 +48,9 @@
 
 def kernel(
     sizes, iters, newton,
-    start_hbm, sens_hbm, kspace_hbm, sampled_hbm, offsets, ahead_hbm, back_hbm,
+    start_hbm, sens_hbm, kspace_hbm, sampled_hbm, offsets_hbm, ahead_hbm, back_hbm,
     out,
-    sens, kspace, sampled, ahead, back,
+    offsets, sens, kspace, sampled, ahead, back,
     field, grad, sums_src, sums, held_src, held, slope_src, slope,
     casorati_src, casorati, shrunk_src, shrunk,
     load_sems, send_sems, recv_sems,
@@ -71,22 +71,24 @@
             (
                 (sampled_hbm, sampled), (start_hbm, field), (sens_hbm, sens),
                 (ahead_hbm, ahead), (kspace_hbm, kspace), (back_hbm, back),
+                (offsets_hbm, offsets),
             )
         )
     ]
     for load in loads:
         load.start()
 
-    def hop_of(i):
-        return nz // 2 + (1 - 2 * (i % 2)) * ((i + 1) // 2)
+    def hop_of(i, flip=0):
+        return nz // 2 + (1 - 2 * ((i + flip) % 2)) * ((i + 1) // 2)
 
     def peers(act, low=0, high=nz, classes=1):
         span = high - low
 
         def body(i, carry):
-            z = (my_z + hop_of(low + i % span)) % nz
             for dx in range(nx // classes):
                 for dy in range(ny):
+                    flip = (dx * ny + dy) % 2 if low == 0 and high == nz else 0
+                    z = (my_z + hop_of(low + i % span, flip)) % nz
                     if classes == 1:
                         x = (my_x + dx) % nx
                     else:
@@ -102,7 +104,7 @@
 
     peers(lambda peer: pl.semaphore_signal(barrier, inc=1, device_id={"tm": peer}))
 
-    for load in loads:
+    for load in loads[:4]:
         load.wait()
     weight = sampled[...].astype(F32)[:, None, :]
 
@@ -145,6 +147,12 @@
                 )
 
             fr, fi = spectra(field[0, here, :], field[1, here, :])
+
+            @pl.when((it == 0) & (c == 0))
+            def _():
+                for load in loads[4:]:
+                    load.wait()
+
             mr = (weight * (fr - kspace[:, 0, here, :].astype(F32))).astype(BF16)
             mi = (weight * (fi - kspace[:, 1, here, :].astype(F32))).astype(BF16)
             misfit = jnp.concatenate(
@@ -310,9 +318,10 @@
         functools.partial(kernel, sizes, iters, newton),
         name="reconstruct",
         out_shape=jax.ShapeDtypeStruct((2, width, length), F32),
-        in_specs=[hbm, hbm, hbm, hbm, pl.BlockSpec(memory_space=pltpu.SMEM), hbm, hbm],
+        in_specs=[hbm] * 7,
         out_specs=vmem,
         scratch_shapes=[
+            pltpu.SMEM(offsets.shape, jnp.int32),
             pltpu.VMEM(sensitivity.shape, BF16),
             pltpu.VMEM(kspace.shape[1:], BF16),
             pltpu.VMEM(sampled.shape[1:], jnp.int32),
@@ -323,12 +332,12 @@
             pltpu.VMEM((iters, 1, LANES), F32),
             pltpu.VMEM((iters, count, 1, LANES), F32),
             *[messages] * 8,
-            pltpu.SemaphoreType.DMA((6,)),
+            pltpu.SemaphoreType.DMA((7,)),
             pltpu.SemaphoreType.DMA((5, iters)),
             pltpu.SemaphoreType.DMA((5, iters)),
         ],
         compiler_params=pltpu.CompilerParams(
-            collective_id=0, has_side_effects=True, vmem_limit_bytes=48 * 2**20
+            collective_id=0, has_side_effects=True, vmem_limit_bytes=67043328
         ),
     )
     result = run(start_image[0], sensitivity, kspace[0], sampled[0], offsets, ahead, back)

time: 112 us -> 105 us (0.938)
  local copies, waits for them, and re-layouts: 7.56 us -> 1.67 us
    unnamed x15 -> x1, local copies, waits for them, and re-layouts: 7.56 us -> 1.67 us
where the time goes in v2:
time: 105 us
  Pallas kernels  103 us (98%)
  local copies, waits for them, and re-layouts  1.67 us (2%)
    pallas_call x1, Pallas kernels, body(): run(start_image[0], sensitivity, kspace[0], sampled[0], offsets, ahead, b...  103 us

profile of v2, /device:TPU:24, one launch (start us, length us, event | category | flops | bytes accessed | tf_op | source)
XLA Modules:
  0.0 104.5 jit_solution(4456202524267981290)
XLA Ops:
  0.0 102.9 %reconstruct.1 = f32[2,128,256]{2,1,0:T(8,128)} custom-call(f32[2,128,256]{2,1,0:T(8,128)} %bitcast.6, bf16[8,2,128,256]{3,2,1,0:T(8,128)(2,1)} %sens_hbm.1, bf16[8,2,128,256]{3,2,1,0:T(8,128)(2,1)} %bitcast.4, s32[8,256]{1,0:T(8,128)} %bitcast.7, s32[2,2]{1,0:T(2,128)} %offsets_hbm.1, bf16[512,512]{1,0:T(8,128)(2,1)} %constant.15.ahead_hbm, ...), custom_call_target="tpu_custom_call" | custom-call | tf_op jit(solution)/shard_map/reconstruct/pallas_call | solution.py:343
  102.9 1.7 %copy.9 = f32[1,2,128,256]{3,2,1,0:T(8,128)} copy(f32[1,2,128,256]{3,2,1,0:T(8,128)} %bitcast.5) | data formatting | bytes 524288

commit v3 on v2

--- a/solution.py
+++ b/solution.py
@@ -13,7 +13,7 @@
 LANES = 128
 PER_TILE = LANES // BS
 ROWS = 128
-EARLY = 0
+EARLY = 1
 CLASSES = 2
 shrink_ratio = 0.5
 epsilon = 1e-06
@@ -35,15 +35,20 @@
 
 def swap_groups(x):
     rows, lanes = x.shape
-    row = lax.broadcasted_iota(jnp.int32, x.shape, 0)
-    lane = lax.broadcasted_iota(jnp.int32, x.shape, 1)
+    x = x.reshape(rows // 8, 8, lanes)
+    row = lax.broadcasted_iota(jnp.int32, x.shape, 1)
+    lane = lax.broadcasted_iota(jnp.int32, x.shape, 2)
     for bit in (1, 2, 4):
         low_row = (row & bit) == 0
         low_lane = (lane & (bit * BS)) == 0
-        from_below = pltpu.roll(pltpu.roll(x, rows - bit, 0), bit * BS, 1)
-        from_above = pltpu.roll(pltpu.roll(x, bit, 0), lanes - bit * BS, 1)
-        x = jnp.where(low_row == low_lane, x, jnp.where(low_row, from_below, from_above))
-    return x
+        other = pltpu.roll(x, bit, 1)
+        if bit < 4:
+            other = jnp.where(low_row, pltpu.roll(x, 8 - bit, 1), other)
+        moved = pltpu.roll(other, bit * BS, 2)
+        if bit < 4:
+            moved = jnp.where(low_lane, pltpu.roll(other, lanes - bit * BS, 2), moved)
+        x = jnp.where(low_row == low_lane, x, moved)
+    return x.reshape(rows, lanes)
 
 
 def kernel(
@@ -317,7 +322,7 @@
     run = pl.pallas_call(
         functools.partial(kernel, sizes, iters, newton),
         name="reconstruct",
-        out_shape=jax.ShapeDtypeStruct((2, width, length), F32),
+        out_shape=pltpu.VMEM((2, width, length), F32),
         in_specs=[hbm] * 7,
         out_specs=vmem,
         scratch_shapes=[
@@ -337,7 +342,7 @@
             pltpu.SemaphoreType.DMA((5, iters)),
         ],
         compiler_params=pltpu.CompilerParams(
-            collective_id=0, has_side_effects=True, vmem_limit_bytes=67043328
+            collective_id=0, has_side_effects=True, vmem_limit_bytes=67043328 - 409600
         ),
     )
     result = run(start_image[0], sensitivity, kspace[0], sampled[0], offsets, ahead, back)

time: 105 us -> 103 us (0.981); the launches traced: 105 us -> 101 us
  Pallas kernels: 103 us -> 100 us
    pallas_call x1, Pallas kernels: 103 us -> 100 us  [body(): run(start_image[0], sensitivity, kspace[0], sampled[0], offsets, ahead, b...]
where the time goes in v3:
time: 103 us; the launch traced here: 101 us
  Pallas kernels  100 us (97%)
    pallas_call x1, Pallas kernels, body(): run(start_image[0], sensitivity, kspace[0], sampled[0], offsets, ahead, b...  100 us

profile of v3, /device:TPU:24, one launch (start us, length us, event | category | flops | bytes accessed | tf_op | source)
XLA Modules:
  0.0 101.2 jit_solution(7413855823659698414)
XLA Ops:
  0.0 100.5 %reconstruct.1 = f32[2,128,256]{2,1,0:T(8,128)S(1)} custom-call(f32[2,128,256]{2,1,0:T(8,128)} %bitcast.6, bf16[8,2,128,256]{3,2,1,0:T(8,128)(2,1)} %sens_hbm.1, bf16[8,2,128,256]{3,2,1,0:T(8,128)(2,1)} %bitcast.5, s32[8,256]{1,0:T(8,128)} %bitcast.7, s32[2,2]{1,0:T(2,128)} %offsets_hbm.1, bf16[512,512]{1,0:T(8,128)(2,1)} %constant.15.ahead_hbm, ...), custom_call_target="tpu_custom_call" | custom-call | tf_op jit(solution)/shard_map/reconstruct/pallas_call | solution.py:348
  100.5 0.7 copy.9

commit v4 on v3

--- a/solution.py
+++ b/solution.py
@@ -88,10 +88,11 @@
 
     def peers(act, low=0, high=nz, classes=1):
         span = high - low
+        across = sorted(range(nx), key=lambda d: -min(d, nx - d))
 
         def body(i, carry):
-            for dx in range(nx // classes):
-                for dy in range(ny):
+            for dx in across if classes == 1 else range(nx // classes):
+                for dy in reversed(range(ny)):
                     flip = (dx * ny + dy) % 2 if low == 0 and high == nz else 0
                     z = (my_z + hop_of(low + i % span, flip)) % nz
                     if classes == 1:
@@ -135,7 +136,7 @@
     def iteration(it, carry):
         def chunk(c, acc):
             num, den = acc
-            r0 = pl.multiple_of(c * ROWS, ROWS)
+            r0 = c * ROWS if isinstance(c, int) else pl.multiple_of(c * ROWS, ROWS)
             here = pl.ds(r0, ROWS)
             sr = sens[:, 0, here, :].astype(F32)
             si = sens[:, 1, here, :].astype(F32)
@@ -177,7 +178,10 @@
             return num, den
 
         zero = jnp.zeros((8, length), F32)
-        num, den = lax.fori_loop(0, width // ROWS, chunk, (zero, zero))
+        if width == ROWS:
+            num, den = chunk(0, (zero, zero))
+        else:
+            num, den = lax.fori_loop(0, width // ROWS, chunk, (zero, zero))
 
         def fold(v):
             v = jnp.sum(v, axis=0, keepdims=True)

time: 103 us -> 103 us (level)
  no operation moved by 1% of the time
where the time goes in v4:
time: 103 us; the launch traced here: 101 us
  Pallas kernels  101 us (98%)
    pallas_call x1, Pallas kernels, body(): run(start_image[0], sensitivity, kspace[0], sampled[0], offsets, ahead, b...  101 us

profile of v4, /device:TPU:24, one launch (start us, length us, event | category | flops | bytes accessed | tf_op | source)
XLA Modules:
  0.0 101.2 jit_solution(14203276005685991586)
XLA Ops:
  0.0 100.5 %reconstruct.1 = f32[2,128,256]{2,1,0:T(8,128)S(1)} custom-call(f32[2,128,256]{2,1,0:T(8,128)} %bitcast.6, bf16[8,2,128,256]{3,2,1,0:T(8,128)(2,1)} %sens_hbm.1, bf16[8,2,128,256]{3,2,1,0:T(8,128)(2,1)} %bitcast.5, s32[8,256]{1,0:T(8,128)} %bitcast.7, s32[2,2]{1,0:T(2,128)} %offsets_hbm.1, bf16[512,512]{1,0:T(8,128)(2,1)} %constant.15.ahead_hbm, ...), custom_call_target="tpu_custom_call" | custom-call | tf_op jit(solution)/shard_map/reconstruct/pallas_call | solution.py:352
  100.5 0.7 copy.9
